TPU v7x, 32 devices: a whole 2x2x4 slice. The times are simulated.
32 devices in a mesh: hst: 4 (over y, x), chip: 8 (over z, core).
Axes of the slice: x: 2, y: 2, z: 4, core: 2. Of those that a mesh axis runs over, the one named last changes fastest.
Arguments:
- resident_row_blocks: bfloat16 [1536, 128, 128], P(('hst', 'chip')), may hold values from -3 to 3
- orphan_blocks: bfloat16 [1024, 128, 128], P(('hst', 'chip')), may hold values from -3 to 3
- home_offsets: int32 [1536, 32, 8], P(('hst', 'chip')), may hold values from 0 to 127
- home_lengths: int32 [1536, 32], P(('hst', 'chip')), may hold values from 1 to 8
- home_samples: int32 [1536, 32], P(('hst', 'chip')), may hold values from 0 to 511
- orphan_offsets: int32 [1024, 32, 8], P(('hst', 'chip')), may hold values from 0 to 127
- orphan_lengths: int32 [1024, 32], P(('hst', 'chip')), may hold values from 1 to 8
- orphan_samples: int32 [1024, 32], P(('hst', 'chip')), may hold values from 0 to 511
- orphan_owner: int32 [1024, 1], P(('hst', 'chip')), may hold values from 0 to 7; in each aligned block of 32 rows (0 to 31, 32 to 63, ...) at most 8 rows name the same one
- dense_inputs: bfloat16 [16384, 13], P(('hst', 'chip')), may hold values from -6 to 6
- labels: int32 [16384], P(('hst', 'chip')), may hold values 0 or 1
- bottom_first: bfloat16 [13, 512], replicated, may hold values from -1.75 to 1.75
- bias_first: float32 [512], replicated, may hold values from -1.5 to 1.5
- bottom_second: bfloat16 [512, 256], replicated, may hold values from -0.375 to 0.375
- bias_second: float32 [256], replicated, may hold values from -1.5 to 1.5
- bottom_third: bfloat16 [256, 128], replicated, may hold values from -0.5 to 0.5
- bias_third: float32 [128], replicated, may hold values from -1.5 to 1.5
- top_hidden: bfloat16 [479, 1024], replicated, may hold values from -0.125 to 0.125
- bias_hidden: float32 [1024], replicated, may hold values from -1.5 to 1.5
- top_logit: bfloat16 [1024, 1], replicated, may hold values from -0.25 to 0.25
- bias_logit: float32 [1], replicated, may hold values from -3 to 3
Outputs:
- rehomed: bfloat16 [2048, 128, 128], P(('hst', 'chip'))
- logits: float32 [16384], P(('hst', 'chip'))
- loss: float32 [], replicated
Inputs may be any that keep to these rules, and one draw needn't show every extreme that they name: `orphan_owner`: among the 32 orphans of one device at most 8 have the same new owner; some holder and owner reach 8.
All inputs are finite; a program needn't handle non-finite values. No bound on the sum of `labels` on one device may be relied on, other than what follows from the above.
Results may differ from a plain program's by a relative error of at most 0.0079.
Values may be sent and summed in bfloat16 or wider, within the bound.
A program may use at most 128 MiB of HBM per device.

v0:
```python
import jax
import jax.numpy as jnp
import numpy as np
from jax import lax
from jax.sharding import PartitionSpec as P

F = 26


def pool_blocks(blocks, offsets, lengths):
    rows = jnp.arange(blocks.shape[1], dtype=jnp.int32)
    counts = jnp.zeros((blocks.shape[0], offsets.shape[1], blocks.shape[1]), jnp.float32)
    for place in range(offsets.shape[2]):
        hit = (offsets[:, :, place, None] == rows[None, None, :]) & (place < lengths)[:, :, None]
        counts = counts + hit.astype(jnp.float32)
    return jnp.einsum(
        "bqr,bre->bqe", counts.astype(jnp.bfloat16), blocks, preferred_element_type=jnp.float32
    ).astype(jnp.bfloat16)


def per_device(
    resident_row_blocks,
    orphan_blocks,
    home_offsets,
    home_lengths,
    home_samples,
    orphan_offsets,
    orphan_lengths,
    orphan_samples,
    orphan_owner,
    dense_inputs,
    labels,
    bottom_first,
    bias_first,
    bottom_second,
    bias_second,
    bottom_third,
    bias_third,
    top_hidden,
    bias_hidden,
    top_logit,
    bias_logit,
):
    hosts = lax.axis_size("hst")
    chips = lax.axis_size("chip")
    devices = hosts * chips
    mine = lax.axis_index(("hst", "chip"))
    home_count = resident_row_blocks.shape[0]
    stranded_block_count = orphan_blocks.shape[0]
    batch_rows = dense_inputs.shape[0]
    width = resident_row_blocks.shape[2]
    slots = (2 * stranded_block_count + chips - 1) // chips
    receive = chips * slots
    owners = orphan_owner[:, 0]
    index = jnp.arange(stranded_block_count, dtype=jnp.int32)
    earlier = index[None, :] < index[:, None]
    rank = jnp.sum(((owners[:, None] == owners[None, :]) & earlier).astype(jnp.int32), axis=1)
    flat = owners * slots + rank
    match = flat[None, :] == jnp.arange(receive, dtype=jnp.int32)[:, None]
    source = jnp.sum(match.astype(jnp.int32) * index[None, :], axis=1)
    filled = jnp.any(match, axis=1)
    outgoing = jnp.where(filled[:, None, None], orphan_blocks[source], jnp.zeros((), jnp.bfloat16))
    rehomed = lax.all_to_all(outgoing, "chip", split_axis=0, concat_axis=0, tiled=True)
    home_ids = mine * home_count + jnp.arange(home_count, dtype=jnp.int32)
    orphan_ids = devices * home_count + mine * stranded_block_count + index
    blocks = jnp.concatenate([resident_row_blocks, orphan_blocks], axis=0)
    offsets = jnp.concatenate([home_offsets, orphan_offsets], axis=0)
    lengths = jnp.concatenate([home_lengths, orphan_lengths], axis=0)
    samples = jnp.concatenate([home_samples, orphan_samples], axis=0)
    block_ids = jnp.concatenate([home_ids, orphan_ids], axis=0)
    first = jax.nn.relu(
        jnp.dot(dense_inputs, bottom_first, preferred_element_type=jnp.float32) + bias_first
    ).astype(jnp.bfloat16)
    second = jax.nn.relu(
        jnp.dot(first, bottom_second, preferred_element_type=jnp.float32) + bias_second
    ).astype(jnp.bfloat16)
    bottom = jax.nn.relu(
        jnp.dot(second, bottom_third, preferred_element_type=jnp.float32) + bias_third
    )
    piece = pool_blocks(blocks, offsets, lengths)
    targets = samples * F + (block_ids % F)[:, None]
    arrived_pieces = lax.all_to_all(piece, ("hst", "chip"), split_axis=1, concat_axis=0, tiled=True)
    arrived_targets = lax.all_to_all(
        targets, ("hst", "chip"), split_axis=1, concat_axis=0, tiled=True
    )
    pooled = jax.ops.segment_sum(
        arrived_pieces.reshape(-1, width).astype(jnp.float32),
        arrived_targets.reshape(-1),
        num_segments=batch_rows * F,
    )
    pooled = pooled.reshape(batch_rows, F, width)
    stacked_vectors = jnp.concatenate([bottom[:, None, :], pooled], axis=1).astype(jnp.bfloat16)
    pairwise_products = jnp.einsum(
        "asu,adu->asd", stacked_vectors, stacked_vectors, preferred_element_type=jnp.float32
    )
    lower_i, lower_j = np.tril_indices(F + 1, -1)
    pairs = pairwise_products[:, lower_i, lower_j]
    feature_vectors = jnp.concatenate([bottom, pairs], axis=1).astype(jnp.bfloat16)
    hidden = jax.nn.relu(
        jnp.dot(feature_vectors, top_hidden, preferred_element_type=jnp.float32) + bias_hidden
    ).astype(jnp.bfloat16)
    logits = jnp.dot(hidden, top_logit, preferred_element_type=jnp.float32)[:, 0] + bias_logit[0]
    local_loss = jnp.sum(jax.nn.softplus(logits) - labels.astype(jnp.float32) * logits)
    loss = lax.psum(local_loss, ("hst", "chip"))
    return (rehomed, logits, loss)


def solution(mesh):
    return jax.shard_map(
        per_device,
        mesh=mesh,
        in_specs=(
            P(("hst", "chip"), None, None),
            P(("hst", "chip"), None, None),
            P(("hst", "chip"), None, None),
            P(("hst", "chip"), None),
            P(("hst", "chip"), None),
            P(("hst", "chip"), None, None),
            P(("hst", "chip"), None),
            P(("hst", "chip"), None),
            P(("hst", "chip"), None),
            P(("hst", "chip"), None),
            P(("hst", "chip")),
            P(),
            P(),
            P(),
            P(),
            P(),
            P(),
            P(),
            P(),
            P(),
            P(),
        ),
        out_specs=(P(("hst", "chip"), None, None), P(("hst", "chip")), P()),
        check_vma=False,
    )
```

profile of v0, /device:TPU:0, one launch (start us, length us, event | category | flops | bytes accessed | tf_op | source)
XLA Modules:
  0.0 152.6 jit_solution(1048473293466418218)
XLA Ops:
  0.7 0.9 copy.91
  1.6 1.4 fusion.63
  3.1 7.3 %all-to-all-start.1 = ((s32[80,32,1]{0,2,1:T(1,128)}), s32[80,32,1]{0,2,1:T(1,128)S(1)}, u32[]{:S(2)}, u32[]{:S(2)}) async-start(s32[80,32,1]{0,2,1:T(1,128)} %fusion.63), calls=%async_computation.1 | async-start | bytes 32768 | tf_op jit(solution)/shard_map/all_to_all | solution.py:83
  10.4 1.0 copy.92
  11.4 1.8 %fusion.57 = (s32[80,32,1]{0,2,1:T(1,128)S(1)}, s32[80,32,1]{0,2,1:T(1,128)S(1)}, s32[80,32,1]{0,2,1:T(1,128)S(1)}, s32[80,32,1]{0,2,1:T(1,128)S(1)}, s32[80,32,...) fusion(s32[48,32,8]{0,2,1:T(8,128)} %param.27, ...), kind=kLoop, calls=%fused_computation.84 | loop fusion | flops 20480 | bytes 163840 | tf_op jit(solution)/shard_map/concatenate | solution.py:67
  14.7 0.8 broadcast_compare_fusion.7
  16.4 9.6 %fusion.12 = bf16[80,32,128]{2,1,0:T(8,128)(2,1)S(1)} fusion(bf16[32,128,128]{2,1,0:T(8,128)(2,1)} %param.26, bf16[48,128,128]{2,1,0:T(8,128)(2,1)} %param.25, s32[80,32]{1,0:T(8,128)S(1)} %copy.108, s32[80,32]{1,0:T(8,128)S(1)} %copy.106, s32[80,32]{1,0:T(8,128)S(1)} %copy.104, s32[80,32]{1,0:T(8,128)S(1)} %copy.102, s32[80,32]{1,0:T(8,128)S(1)} %copy.100, ...), kind=kOutput, calls=%fused_computation.18 | convolution fusion | flops 96010240 | bytes 3379200 | tf_op jit(solution)/shard_map/bqr,bre->bqe/dot_general | solution.py:16
  26.0 1.1 copy.110
  27.1 5.9 %all-to-all-start.2 = ((bf16[80,32,128]{2,0,1:T(8,128)(2,1)}), bf16[80,32,128]{2,0,1:T(8,128)(2,1)}, u32[]{:S(2)}, u32[]{:S(2)}) async-start(bf16[80,32,128]{2,0,1:T(8,128)(2,1)} %copy.110), calls=%async_computation.2 | async-start | bytes 1310720 | tf_op jit(solution)/shard_map/all_to_all | solution.py:82
  33.4 2.2 %gather_fusion = bf16[64,128,128]{2,1,0:T(8,128)(2,1)S(1)} fusion(bf16[32,128,128]{2,1,0:T(8,128)(2,1)} %param.26, s32[1024]{0:T(1024)S(1)} %pad_clamp_fusion), kind=kCustom, calls=%fused_computation | custom fusion | bytes 4194560 | tf_op jit(solution)/shard_map/gather | solution.py:62
  35.7 1.5 %broadcast_select_fusion = bf16[64,128,128]{2,1,0:T(8,128)(2,1)} fusion(bf16[64,128,128]{2,1,0:T(8,128)(2,1)S(1)} %gather_fusion, pred[64]{0:T(512)(128)(4,1)S(1)} %fusion.64), kind=kLoop, calls=%fused_computation.14 | loop fusion | flops 1048576 | bytes 4194368 | tf_op jit(solution)/shard_map/jit(_where)/select_n | solution.py:62
  37.3 14.9 %all-to-all-done.2 = bf16[80,32,128]{2,0,1:T(8,128)(2,1)} async-done(((bf16[80,32,128]{2,0,1:T(8,128)(2,1)}), bf16[80,32,128]{2,0,1:T(8,128)(2,1)}, u32[]{:S(2)}, u32[]{:S(2)}) %all-to-all-start.2) | async-done | bytes 655392 | tf_op jit(solution)/shard_map/all_to_all | solution.py:82
  52.1 4.3 %all-to-all-start = ((bf16[64,128,128]{2,1,0:T(8,128)(2,1)}), bf16[64,128,128]{2,1,0:T(8,128)(2,1)}, u32[]{:S(2)}, u32[]{:S(2)}) async-start(bf16[64,128,128]{2,1,0:T(8,128)(2,1)} %broadcast_select_fusion), calls=%async_computation | async-start | bytes 4194304 | tf_op jit(solution)/shard_map/all_to_all | solution.py:63
  58.2 1.2 bitcast_convert_fusion
  59.4 17.4 %scatter_custom_fusion = f32[13312,128]{1,0:T(8,128)} fusion(s32[2560]{0:T(1024)S(1)} %reshape.262, f32[2560,128]{1,0:T(8,128)S(1)} %bitcast.38, f32[]{:T(128)} %constant.27.clone.1), kind=kCustom, calls=%fused_computation.7 | custom fusion | flops 327680 | bytes 6815748 | tf_op jit(solution)/shard_map/scatter-add | solution.py:86
  76.7 4.4 %convert.16 = bf16[13312,128]{1,0:T(8,128)(2,1)} convert(f32[13312,128]{1,0:T(8,128)} %scatter_custom_fusion) | non-fusion elementwise | flops 1703936 | bytes 10223616 | tf_op jit(solution)/shard_map/convert.7
  81.1 6.5 %reshape.242 = bf16[512,26,128]{2,1,0:T(8,128)(2,1)} reshape(bf16[13312,128]{1,0:T(8,128)(2,1)} %convert.16) | data formatting | bytes 6815744 | tf_op jit(solution)/shard_map/reshape | solution.py:91
  87.6 8.2 %fusion = bf16[512,27,27]{2,1,0:T(8,128)(2,1)} fusion(bf16[512,26,128]{2,1,0:T(8,128)(2,1)} %reshape.242, bf16[512,1,128]{2,1,0:T(2,128)(2,1)S(1)} %copy.111), kind=kOutput, calls=%fused_computation.3 | convolution fusion | flops 102629376 | bytes 4285440 | tf_op jit(solution)/shard_map/asu,adu->asd/dot_general | solution.py:93
  95.8 6.0 %copy.112 = bf16[512,27,27]{0,2,1:T(8,128)(2,1)S(1)} copy(bf16[512,27,27]{2,1,0:T(8,128)(2,1)} %fusion) | data formatting | bytes 1492992 | tf_op jit(solution)/shard_map/asu,adu->asd/dot_general | solution.py:93
  101.8 5.5 %gather_fusion.1 = bf16[351,512]{1,0:T(8,128)(2,1)S(1)} fusion(bf16[512,27,27]{0,2,1:T(8,128)(2,1)S(1)} %copy.112, s32[351]{0:T(512)S(1)} %copy-done.1), kind=kCustom, calls=%fused_computation.1 | custom fusion | bytes 721656 | tf_op jit(solution)/shard_map/gather | solution.py:97
  107.3 0.9 fusion.10
  108.2 1.3 fusion.67
  109.5 39.9 %psum.7 = f32[]{:T(128)} all-reduce(f32[]{:T(128)} %get-tuple-element.3), channel_id=1, replica_groups=mesh['hst'=4,'chip'=8] {'hst','chip'}, use_global_device_ids=true, to_apply=%region_5.6 | all-reduce | flops 1 | bytes 8 | tf_op jit(solution)/shard_map/psum | solution.py:104
  149.4 3.2 %copy.115 = bf16[64,128,128]{2,1,0:T(8,128)(2,1)} copy(bf16[64,128,128]{2,1,0:T(8,128)(2,1)} %all-to-all-done) | data formatting | bytes 4194304
  (60 shorter events, 3.8 us)
Async XLA Ops:
  0.6 106.6 %copy-start = (bf16[479,1024]{1,0:T(8,128)(2,1)S(1)}, bf16[479,1024]{1,0:T(8,128)(2,1)}, u32[]{:S(2)}) copy-start(bf16[479,1024]{1,0:T(8,128)(2,1)} %param.42) | copy-start | bytes 2942980
  3.1 24.1 %all-to-all-start.1 = ((s32[80,32,1]{0,2,1:T(1,128)}), s32[80,32,1]{0,2,1:T(1,128)S(1)}, u32[]{:S(2)}, u32[]{:S(2)}) async-start(s32[80,32,1]{0,2,1:T(1,128)} %fusion.63), calls=%async_computation.1 | async-start | bytes 32768 | tf_op jit(solution)/shard_map/all_to_all | solution.py:83
  26.0 7.1 %copy-start.12 = (s32[32,1]{0,1:T(1,128)S(1)}, s32[32,1]{0,1:T(1,128)}, u32[]{:S(2)}) copy-start(s32[32,1]{0,1:T(1,128)} %param.33) | copy-start | bytes 388
  27.1 25.0 %all-to-all-start.2 = ((bf16[80,32,128]{2,0,1:T(8,128)(2,1)}), bf16[80,32,128]{2,0,1:T(8,128)(2,1)}, u32[]{:S(2)}, u32[]{:S(2)}) async-start(bf16[80,32,128]{2,0,1:T(8,128)(2,1)} %copy.110), calls=%async_computation.2 | async-start | bytes 1310720 | tf_op jit(solution)/shard_map/all_to_all | solution.py:82
  37.2 19.3 %copy-start.5 = (bf16[512,256]{1,0:T(8,128)(2,1)S(1)}, bf16[512,256]{1,0:T(8,128)(2,1)}, u32[]{:S(2)}) copy-start(bf16[512,256]{1,0:T(8,128)(2,1)} %param.38) | copy-start | bytes 786436
  37.2 19.3 %copy-start.6 = (bf16[512,13]{0,1:T(8,128)(2,1)S(1)}, bf16[512,13]{0,1:T(8,128)(2,1)}, u32[]{:S(2)}) copy-start(bf16[512,13]{0,1:T(8,128)(2,1)} %param.34) | copy-start | bytes 39940
  37.2 19.3 %copy-start.7 = (bf16[13,512]{1,0:T(8,128)(2,1)S(1)}, bf16[13,512]{1,0:T(8,128)(2,1)}, u32[]{:S(2)}) copy-start(bf16[13,512]{1,0:T(8,128)(2,1)} %param.36) | copy-start | bytes 39940
  37.2 19.3 %copy-start.10 = (f32[512]{0:T(512)S(1)}, f32[512]{0:T(512)}, u32[]{:S(2)}) copy-start(f32[512]{0:T(512)} %param.37) | copy-start | bytes 6148
  37.2 19.3 %copy-start.11 = (f32[256]{0:T(256)S(1)}, f32[256]{0:T(256)}, u32[]{:S(2)}) copy-start(f32[256]{0:T(256)} %param.39) | copy-start | bytes 3076
  37.2 19.8 %copy-start.2 = (bf16[256,128]{1,0:T(8,128)(2,1)S(1)}, bf16[256,128]{1,0:T(8,128)(2,1)}, u32[]{:S(2)}) copy-start(bf16[256,128]{1,0:T(8,128)(2,1)} %param.40) | copy-start | bytes 196612
  37.2 19.8 %copy-start.4 = (f32[128]{0:T(128)S(1)}, f32[128]{0:T(128)}, u32[]{:S(2)}) copy-start(f32[128]{0:T(128)} %param.41) | copy-start | bytes 1540
  52.1 97.3 %all-to-all-start = ((bf16[64,128,128]{2,1,0:T(8,128)(2,1)}), bf16[64,128,128]{2,1,0:T(8,128)(2,1)}, u32[]{:S(2)}, u32[]{:S(2)}) async-start(bf16[64,128,128]{2,1,0:T(8,128)(2,1)} %broadcast_select_fusion), calls=%async_computation | async-start | bytes 4194304 | tf_op jit(solution)/shard_map/all_to_all | solution.py:63
  95.8 6.0 %copy-start.1 = (s32[351]{0:T(512)S(1)}, s32[351]{0:T(512)}, u32[]{:S(2)}) copy-start(s32[351]{0:T(512)} %constant.104) | copy-start | bytes 4216
  101.8 5.5 %copy-start.8 = (bf16[1024,1]{0,1:T(2,128)(2,1)S(1)}, bf16[1024,1]{0,1:T(2,128)(2,1)}, u32[]{:S(2)}) copy-start(bf16[1024,1]{0,1:T(2,128)(2,1)} %param.44) | copy-start | bytes 6148
  101.8 5.5 %copy-start.9 = (f32[1024]{0:T(1024)S(1)}, f32[1024]{0:T(1024)}, u32[]{:S(2)}) copy-start(f32[1024]{0:T(1024)} %param.43) | copy-start | bytes 12292
  107.3 0.9 copy-start.3
where the time goes:
time: 154 us; the launch traced here: 153 us
  blocking collectives  39.9 us (26%)
  other arithmetic  30.3 us (20%)
  local copies, waits for them, and re-layouts  28.9 us (19%)
  matrix products  19.3 us (13%)
  starting transfers between devices  17.6 us (11%)
  waiting for transfers between devices  14.9 us (10%)
  between operations  1.67 us (1%)
    psum x1, blocking collectives, per_device(): loss = lax.psum(local_loss, ('hst', 'chip'))  39.9 us
    scatter-add x1, other arithmetic, per_device(): jax.ops.segment_sum(arrived_pieces.reshape(-1, width).astype(jnp.float32)...  17.4 us
    all_to_all x1, waiting for transfers between devices, per_device(): lax.all_to_all(piece, ('hst', 'chip'), split_axis=1, concat_axis=0, tiled...  14.9 us
    dot_general x1, matrix products, pool_blocks(): jnp.einsum('bqr,bre->bqe', counts.astype(jnp.bfloat16), blocks, preferred...  9.58 us
    dot_general x1, matrix products, per_device(): jnp.einsum('asu,adu->asd', stacked_vectors, stacked_vectors, preferred_el...  8.15 us
    all_to_all x1, starting transfers between devices, per_device(): lax.all_to_all(targets, ('hst', 'chip'), split_axis=1, concat_axis=0, til...  7.33 us
    reshape x1, local copies, waits for them, and re-layouts, per_device(): pooled = pooled.reshape(batch_rows, F, width)  6.5 us
    dot_general x1, local copies, waits for them, and re-layouts, per_device(): jnp.einsum('asu,adu->asd', stacked_vectors, stacked_vectors, preferred_el...  5.96 us
  transfers between devices with their start and end apart: 3, of which 1 were waited for; matrix products, arithmetic and copies ran while one was open for 48% of the time, Pallas kernels for 0%

commit v1 on v0

v1 whole, which is shorter than its diff:
```python
import functools

import jax
import jax.numpy as jnp
from jax import lax
from jax.experimental import pallas as pl
from jax.experimental.pallas import tpu as pltpu
from jax.sharding import PartitionSpec as P

F = 26
SLAB = 32
VM = pltpu.VMEM
F32, BF16, I32 = jnp.float32, jnp.bfloat16, jnp.int32


def cost(flops, bytes_accessed):
    return pl.CostEstimate(flops=flops, bytes_accessed=bytes_accessed, transcendentals=0)


def nt(a, b):
    return lax.dot_general(a, b, (((1,), (1,)), ((), ())), preferred_element_type=F32)


def mm(a, b):
    return jnp.dot(a, b, preferred_element_type=F32)


def place_kernel(slots, owner_ref, blocks_ref, out_ref, used):
    chips = out_ref.shape[0] // slots
    out_ref[...] = jnp.zeros_like(out_ref)
    for c in range(chips):
        used[c] = 0

    def step(i, carry):
        c = owner_ref[i]
        rank = used[c]
        used[c] = rank + 1
        out_ref[c * slots + rank] = blocks_ref[i]
        return carry

    lax.fori_loop(0, blocks_ref.shape[0], step, 0)


def place(owners, blocks, chips, slots):
    shape = (chips * slots,) + blocks.shape[1:]
    return pl.pallas_call(
        functools.partial(place_kernel, slots),
        out_shape=jax.ShapeDtypeStruct(shape, blocks.dtype),
        in_specs=[pl.BlockSpec(memory_space=pltpu.SMEM), pl.BlockSpec(memory_space=VM)],
        out_specs=pl.BlockSpec(memory_space=VM),
        scratch_shapes=[pltpu.SMEM((chips,), I32)],
        cost_estimate=cost(1000, 3 * blocks.size * 2),
        name="place",
    )(owners, blocks)


def pool_kernel(peers, stride, off_ref, samp_ref, home_ref, orph_ref, out_ref, rows_ref):
    homes, height = home_ref.shape[0], home_ref.shape[1]
    count = homes + orph_ref.shape[0]
    per = 128 // peers
    row = lax.broadcasted_iota(I32, (height, 128), 0)
    rows_ref[...] = jnp.zeros_like(rows_ref)
    samp = samp_ref[...]
    rows_ref[pl.ds(count, peers, stride=stride), :] = (samp // 256).astype(F32)
    rows_ref[pl.ds(count + 1, peers, stride=stride), :] = (samp % 256).astype(F32)

    def group(block_ref, base):
        def step(g, carry):
            first = base + g * per
            lanes = pl.ds(pl.multiple_of(first * peers, 128), 128)
            hits = jnp.zeros((height, 128), F32)
            for place_ in range(off_ref.shape[0]):
                hits = hits + (row == off_ref[place_:place_ + 1, lanes]).astype(F32)
            counts = hits.T.astype(BF16)
            for k in range(per):
                piece = mm(counts[k * peers:(k + 1) * peers], block_ref[g * per + k])
                rows_ref[pl.ds(first + k, peers, stride=stride), :] = piece
            return carry

        lax.fori_loop(0, block_ref.shape[0] // per, step, 0, unroll=2)

    group(home_ref, 0)
    group(orph_ref, homes)
    out_ref[...] = rows_ref[...].astype(BF16)


def pool(off, samp, home, orph, peers, stride):
    width = home.shape[2]
    return pl.pallas_call(
        functools.partial(pool_kernel, peers, stride),
        out_shape=jax.ShapeDtypeStruct((peers * stride, width), BF16),
        in_specs=[pl.BlockSpec(memory_space=VM)] * 4,
        out_specs=pl.BlockSpec(memory_space=VM),
        scratch_shapes=[VM((peers * stride, width), F32)],
        cost_estimate=cost(2 * peers * (home.size + orph.size), 4 * home.size),
        name="pool",
    )(off, samp, home, orph)


def top_kernel(
    homes, orphs, depth,
    arr_ref, samp_ref, dense_ref, w1_ref, b1_ref, w2_ref, b2_ref, w3_ref, b3_ref,
    wt_ref, bh_ref, wl_ref, bl_ref, label_ref,
    logit_ref, loss_ref,
    pieces, slab, gram, wpad, wexp,
):
    peers = arr_ref.shape[0]
    batch = dense_ref.shape[0]
    inter = wt_ref.shape[0]
    total = peers * (homes + orphs)

    whole = inter // 16 * 16
    wpad[whole:, :] = jnp.zeros((wpad.shape[0] - whole, wpad.shape[1]), BF16)
    wpad[0:inter, :] = wt_ref[...]
    slot = lax.broadcasted_iota(I32, (SLAB * SLAB, wpad.shape[0]), 0)
    i, j = slot // SLAB, slot % SLAB
    column = lax.broadcasted_iota(I32, slot.shape, 1)
    pick = (column == 128 + i * (i - 1) // 2 + j) & (j < i) & (i <= F)
    wexp[...] = mm(jnp.where(pick, 1.0, 0.0).astype(BF16), wpad[...]).astype(BF16)

    first = jnp.maximum(mm(dense_ref[...], w1_ref[...]) + b1_ref[...], 0.0).astype(BF16)
    second = jnp.maximum(mm(first, w2_ref[...]) + b2_ref[...], 0.0).astype(BF16)
    bottom = jnp.maximum(mm(second, w3_ref[...]) + b3_ref[...], 0.0)
    slab[0] = bottom
    slab[F + 1:] = jnp.zeros((SLAB - F - 1,) + slab.shape[1:], F32)

    pieces[total:, :] = jnp.zeros((pieces.shape[0] - total, pieces.shape[1]), F32)

    def settle(p, carry):
        pieces[pl.ds(pl.multiple_of(p * homes, 8), homes), :] = arr_ref[p, 0:homes].astype(F32)
        pieces[pl.ds(pl.multiple_of(peers * homes + p * orphs, 8), orphs), :] = (
            arr_ref[p, homes:homes + orphs].astype(F32))
        return carry

    lax.fori_loop(0, peers, settle, 0, unroll=2)

    sample = lax.broadcasted_iota(I32, (batch, depth), 0)
    for f in range(F):
        mine = pieces[pl.ds(f, depth, stride=F), :].astype(BF16)
        hot = jnp.where(sample == samp_ref[f:f + 1, :], 1.0, 0.0).astype(BF16)
        slab[f + 1] = mm(hot, mine)

    edge = SLAB * 8
    same = (lax.broadcasted_iota(I32, (edge, edge), 0) % 8) == (
        lax.broadcasted_iota(I32, (edge, edge), 1) % 8)

    def products(g, carry):
        halves = []
        for k in range(2):
            at = pl.ds(pl.multiple_of(g * 16 + k * 8, 8), 8)
            x = slab[:, at, :].reshape(edge, slab.shape[2]).astype(BF16)
            halves.append(jnp.where(same, nt(x, x), 0.0).reshape(SLAB, 8, edge))
        both = jnp.concatenate(halves, axis=1).astype(BF16)
        gram[:, pl.ds(pl.multiple_of(g * 16, 16), 16), :] = both
        return carry

    lax.fori_loop(0, batch // 16, products, 0, unroll=2)

    lane_j = lax.broadcasted_iota(I32, (edge, edge), 0) // 8
    out_lane = lax.broadcasted_iota(I32, (edge, edge), 1)
    features = []
    for h in range(SLAB // 8):
        acc = None
        for k in range(8):
            i_ = h * 8 + k
            if i_ < 1 or i_ > F:
                continue
            live = 128 if i_ <= 16 else edge
            fold = jnp.where(lane_j + k * SLAB == out_lane, 1.0, 0.0).astype(BF16)
            term = mm(gram[i_, :, 0:live], fold[0:live])
            acc = term if acc is None else acc + term
        features.append(acc.astype(BF16))
    bottom = slab[0].astype(BF16)

    part = jnp.zeros((batch, 128), F32)
    step = 256
    for n in range(0, wt_ref.shape[1], step):
        pre = mm(bottom, wpad[0:128, n:n + step])
        for h in range(SLAB // 8):
            pre = pre + mm(features[h], wexp[h * 256:(h + 1) * 256, n:n + step])
        hidden = jnp.maximum(pre + bh_ref[:, n:n + step], 0.0).astype(BF16).astype(F32)
        scaled = hidden * wl_ref[:, n:n + step]
        part = part + scaled[:, 0:128] + scaled[:, 128:256]
    logits = jnp.sum(part.T, axis=0, keepdims=True) + bl_ref[0]
    logit_ref[...] = logits
    soft = jnp.maximum(logits, 0.0) + jnp.log1p(jnp.exp(-jnp.abs(logits)))
    loss = jnp.sum(soft - label_ref[...].astype(F32) * logits, axis=1, keepdims=True)
    loss_ref[...] = jnp.broadcast_to(loss, loss_ref.shape)


def top(homes, orphs, depth, arrived, samp, dense, w1, b1, w2, b2, w3, b3, wt, bh, wl, bl, labels):
    peers, _, width = arrived.shape
    batch = dense.shape[0]
    vmem = pl.BlockSpec(memory_space=VM)
    return pl.pallas_call(
        functools.partial(top_kernel, homes, orphs, depth),
        out_shape=(
            jax.ShapeDtypeStruct((1, batch), F32),
            jax.ShapeDtypeStruct((peers, 128), F32),
        ),
        in_specs=[vmem] * 12 + [pl.BlockSpec(memory_space=pltpu.SMEM), vmem],
        out_specs=(vmem, vmem),
        scratch_shapes=[
            VM((F * depth, width), F32),
            VM((SLAB, batch, width), F32),
            VM((SLAB, batch, SLAB * 8), BF16),
            VM((512, wt.shape[1]), BF16),
            VM((SLAB * SLAB, wt.shape[1]), BF16),
        ],
        cost_estimate=cost(8_000_000_000, 8_000_000),
        name="top",
    )(arrived, samp, dense, w1, b1, w2, b2, w3, b3, wt, bh, wl, bl, labels)


def per_device(
    resident_row_blocks,
    orphan_blocks,
    home_offsets,
    home_lengths,
    home_samples,
    orphan_offsets,
    orphan_lengths,
    orphan_samples,
    orphan_owner,
    dense_inputs,
    labels,
    bottom_first,
    bias_first,
    bottom_second,
    bias_second,
    bottom_third,
    bias_third,
    top_hidden,
    bias_hidden,
    top_logit,
    bias_logit,
):
    chips = lax.axis_size("chip")
    devices = lax.axis_size("hst") * chips
    everyone = ("hst", "chip")
    homes, orphs = resident_row_blocks.shape[0], orphan_blocks.shape[0]
    height, width = resident_row_blocks.shape[1:]
    batch = dense_inputs.shape[0]
    slots = (2 * orphs + chips - 1) // chips
    count = homes + orphs
    stride = -(-(count + 2) // 16) * 16

    outgoing = place(orphan_owner[:, 0], orphan_blocks, chips, slots)
    rehomed = lax.all_to_all(outgoing, "chip", split_axis=0, concat_axis=0, tiled=True)

    offsets = jnp.concatenate([home_offsets, orphan_offsets], axis=0)
    lengths = jnp.concatenate([home_lengths, orphan_lengths], axis=0)
    samples = jnp.concatenate([home_samples, orphan_samples], axis=0)
    live = jnp.arange(offsets.shape[2], dtype=I32) < lengths[:, :, None]
    off = jnp.where(live, offsets, height).transpose(2, 0, 1).reshape(offsets.shape[2], -1)
    samp = jnp.pad(samples.T, ((0, 0), (0, 128 - count)))

    packed = pool(off, samp, resident_row_blocks, orphan_blocks, devices, stride)
    packed = packed.reshape(devices, stride, width)
    arrived = lax.all_to_all(packed, everyone, split_axis=0, concat_axis=0, tiled=True)

    total = devices * count
    depth = -(-total // (F * 128)) * 128
    where = (arrived[:, count, :count].astype(F32) * 256.0
             + arrived[:, count + 1, :count].astype(F32)).astype(I32)
    where = jnp.concatenate([where[:, :homes].reshape(-1), where[:, homes:].reshape(-1)])
    where = jnp.pad(where, (0, F * depth - total), constant_values=-1).reshape(depth, F).T

    logits, loss = top(
        homes, orphs, depth, arrived, where, dense_inputs,
        bottom_first, bias_first[None], bottom_second, bias_second[None],
        bottom_third, bias_third[None], top_hidden, bias_hidden[None],
        top_logit.T.astype(F32), bias_logit, labels[None],
    )
    losses = lax.all_to_all(loss[:, None, :], everyone, split_axis=0, concat_axis=0, tiled=True)
    return rehomed, logits[0], jnp.sum(losses[:, 0, 0])


def solution(mesh):
    both = ("hst", "chip")
    three, two = P(both, None, None), P(both, None)
    return jax.shard_map(
        per_device,
        mesh=mesh,
        in_specs=(three, three, three, two, two, three, two, two, two, two, P(both)) + (P(),) * 10,
        out_specs=(three, P(both), P()),
        check_vma=False,
    )
```

time: 154 us -> 122 us (0.79)
  waiting for transfers between devices: 14.9 us -> 72.1 us
  blocking collectives: 39.9 us -> 0 us
  other arithmetic: 30.3 us -> 3.87 us
  Pallas kernels: 0 us -> 23.1 us
  local copies, waits for them, and re-layouts: 28.9 us -> 7.3 us
  matrix products: 19.3 us -> 0 us
  starting transfers between devices: 17.6 us -> 13.4 us
    all_to_all x1, waiting for transfers between devices: 0.01 us -> 48.3 us  [per_device(): lax.all_to_all(outgoing, 'chip', split_axis=0, concat_axis=0, tiled=True)]
    psum x1 -> x0, blocking collectives: 39.9 us -> none  [per_device(): loss = lax.psum(local_loss, ('hst', 'chip'))]
    pallas_call x0 -> x3, Pallas kernels: none -> 23.1 us  [the longest x1 13.8 us: top(): pl.pallas_call(functools.partial(top_kernel, homes, orphs, depth), out_sh...]
    dot_general x5 -> x0, matrix products: 19.3 us -> none  [the longest x1 9.58 us: pool_blocks(): jnp.einsum('bqr,bre->bqe', counts.astype(jnp.bfloat16), blocks, preferred...]
    scatter-add x1 -> x0, other arithmetic: 17.4 us -> none  [per_device(): jax.ops.segment_sum(arrived_pieces.reshape(-1, width).astype(jnp.float32)...]
    all_to_all x2, waiting for transfers between devices: 14.9 us -> 23.8 us  [the longest x1 19.8 us: per_device(): lax.all_to_all(packed, everyone, split_axis=0, concat_axis=0, tiled=True)]
    gather x2 -> x0, local copies, waits for them, and re-layouts: 7.64 us -> none  [the longest x1 5.46 us: per_device(): pairs = pairwise_products[:, lower_i, lower_j]]
    dot_general x1 -> x0, local copies, waits for them, and re-layouts: 5.96 us -> none  [per_device(): jnp.einsum('asu,adu->asd', stacked_vectors, stacked_vectors, preferred_el...]
  transfers between devices with their start and end apart: 3 -> 3, of which waited for: 1 -> 3; matrix products, arithmetic and copies ran while one was open for 48% -> 2% of each run, Pallas kernels for 0% -> 3%
where the time goes in v1:
time: 122 us; the launch traced here: 121 us
  waiting for transfers between devices  72.1 us (59%)
  Pallas kernels  23.1 us (19%)
  starting transfers between devices  13.4 us (11%)
  local copies, waits for them, and re-layouts  7.3 us (6%)
  other arithmetic  3.87 us (3%)
  between operations  1.37 us (1%)
    all_to_all x1, waiting for transfers between devices, per_device(): lax.all_to_all(outgoing, 'chip', split_axis=0, concat_axis=0, tiled=True)  48.3 us
    all_to_all x1, waiting for transfers between devices, per_device(): lax.all_to_all(packed, everyone, split_axis=0, concat_axis=0, tiled=True)  19.8 us
    pallas_call x1, Pallas kernels, top(): pl.pallas_call(functools.partial(top_kernel, homes, orphs, depth), out_sh...  13.8 us
    all_to_all x1, starting transfers between devices, per_device(): lax.all_to_all(packed, everyone, split_axis=0, concat_axis=0, tiled=True)  7.33 us
    pallas_call x1, Pallas kernels, pool(): pl.pallas_call(functools.partial(pool_kernel, peers, stride), out_shape=j...  6.19 us
    unnamed x11, local copies, waits for them, and re-layouts  4.7 us
    all_to_all x1, waiting for transfers between devices, per_device(): lax.all_to_all(loss[:, None, :], everyone, split_axis=0, concat_axis=0, t...  3.99 us
    all_to_all x1, starting transfers between devices, per_device(): lax.all_to_all(outgoing, 'chip', split_axis=0, concat_axis=0, tiled=True)  3.61 us
  transfers between devices with their start and end apart: 3, of which 3 were waited for; matrix products, arithmetic and copies ran while one was open for 2% of the time, Pallas kernels for 3%

profile of v1, /device:TPU:0, one launch (start us, length us, event | category | flops | bytes accessed | tf_op | source)
XLA Modules:
  0.0 121.2 jit_solution(519393038851798484)
XLA Ops:
  0.6 1.0 copy.36
  1.6 0.8 copy.35
  2.4 0.8 pad_add_fusion
  3.2 1.0 fusion
  4.2 0.2 copy.37
  4.4 0.8 reshape.42.off_ref
  5.2 0.8 copy.38
  6.0 0.8 add_bitcast_fusion
  6.8 0.6 pad.8.samp_ref
  7.4 6.2 %pool.1 = bf16[3072,128]{1,0:T(8,128)(2,1)} custom-call(s32[8,2560]{1,0:T(8,128)} %reshape.42.off_ref, s32[32,128]{1,0:T(8,128)} %pad.8.samp_ref, bf16[48,128,128]{2,1,0:T(8,128)(2,1)} %home_ref.1, bf16[32,128,128]{2,1,0:T(8,128)(2,1)} %orph_ref.1), custom_call_target="tpu_custom_call" | custom-call | flops 83886080 | bytes 3145728 | tf_op jit(solution)/shard_map/pool/pallas_call | solution.py:89
  13.6 7.3 %all-to-all-start.1 = ((bf16[32,96,128]{2,1,0:T(8,128)(2,1)}), bf16[32,96,128]{2,1,0:T(8,128)(2,1)S(1)}, u32[]{:S(2)}, u32[]{:S(2)}) async-start(bf16[32,96,128]{2,1,0:T(8,128)(2,1)} %bitcast.21), calls=%async_computation.1 | async-start | bytes 1572864 | tf_op jit(solution)/shard_map/all_to_all | solution.py:260
  20.9 0.8 copy.40.dense_ref
  22.4 0.6 bitcast_convert_fusion.wl_ref
  23.0 19.8 %all-to-all-done.1.arr_ref = bf16[32,96,128]{2,1,0:T(8,128)(2,1)S(1)} async-done(((bf16[32,96,128]{2,1,0:T(8,128)(2,1)}), bf16[32,96,128]{2,1,0:T(8,128)(2,1)S(1)}, u32[]{:S(2)}, u32[]{:S(2)}) %all-to-all-start.1) | async-done | bytes 786464 | tf_op jit(solution)/shard_map/all_to_all | solution.py:260
  43.1 0.1 reshape.46
  43.2 0.7 copy.39
  43.9 13.8 %top.1 = (f32[1,512]{1,0:T(1,128)}, f32[32,128]{1,0:T(8,128)}) custom-call(bf16[32,96,128]{2,1,0:T(8,128)(2,1)} %copy-done, s32[26,128]{1,0:T(8,128)} %bitcast.24, bf16[512,13]{1,0:T(8,128)(2,1)} %copy.40.dense_ref, bf16[13,512]{1,0:T(8,128)(2,1)} %w1_ref.1, f32[1,512]{1,0:T(1,128)} %bitcast.28, bf16[512,256]{1,0:T(8,128)(2,1)} %w2_ref.1, ...), custom_call_target="tpu_custom_call" | custom-call | flops 8000000000 | bytes 8000000 | tf_op jit(solution)/shard_map/top/pallas_call | solution.py:195
  57.6 2.5 %all-to-all-start.2 = ((f32[32,1,128]{2,1,0:T(1,128)}), f32[32,1,128]{2,1,0:T(1,128)S(1)}, u32[]{:S(2)}, u32[]{:S(2)}) async-start(f32[32,1,128]{2,1,0:T(1,128)} %bitcast.25), calls=%async_computation.2 | async-start | bytes 32768 | tf_op jit(solution)/shard_map/all_to_all | solution.py:275
  60.2 3.2 %place.1 = bf16[64,128,128]{2,1,0:T(8,128)(2,1)} custom-call(s32[32]{0:T(128)} %bitcast.26, bf16[32,128,128]{2,1,0:T(8,128)(2,1)} %orph_ref.1), custom_call_target="tpu_custom_call" | custom-call | flops 1000 | bytes 3145728 | tf_op jit(solution)/shard_map/place/pallas_call | solution.py:46
  63.3 4.0 %all-to-all-done.2 = f32[32,1,128]{2,1,0:T(1,128)S(1)} async-done(((f32[32,1,128]{2,1,0:T(1,128)}), f32[32,1,128]{2,1,0:T(1,128)S(1)}, u32[]{:S(2)}, u32[]{:S(2)}) %all-to-all-start.2) | async-done | bytes 16416 | tf_op jit(solution)/shard_map/all_to_all | solution.py:275
  67.3 3.6 %all-to-all-start = ((bf16[64,128,128]{2,1,0:T(8,128)(2,1)}), bf16[64,128,128]{2,1,0:T(8,128)(2,1)S(1)}, u32[]{:S(2)}, u32[]{:S(2)}) async-start(bf16[64,128,128]{2,1,0:T(8,128)(2,1)} %place.1), calls=%async_computation | async-start | bytes 4194304 | tf_op jit(solution)/shard_map/all_to_all | solution.py:249
  70.9 0.6 slice_reduce_fusion
  71.6 48.3 %all-to-all-done = bf16[64,128,128]{2,1,0:T(8,128)(2,1)S(1)} async-done(((bf16[64,128,128]{2,1,0:T(8,128)(2,1)}), bf16[64,128,128]{2,1,0:T(8,128)(2,1)S(1)}, u32[]{:S(2)}, u32[]{:S(2)}) %all-to-all-start) | async-done | bytes 2097184 | tf_op jit(solution)/shard_map/all_to_all | solution.py:249
  119.9 1.3 %copy.44 = bf16[64,128,128]{2,1,0:T(8,128)(2,1)} copy(bf16[64,128,128]{2,1,0:T(8,128)(2,1)S(1)} %all-to-all-done) | data formatting | bytes 4194304
  (12 shorter events, 0.3 us)
Async XLA Ops:
  7.4 13.5 %copy-start.1 = (bf16[512,13]{0,1:T(8,128)(2,1)S(1)}, bf16[512,13]{0,1:T(8,128)(2,1)}, u32[]{:S(2)}) copy-start(bf16[512,13]{0,1:T(8,128)(2,1)} %param.30) | copy-start | bytes 39940
  7.4 15.0 %copy-start.2 = (bf16[1024,1]{0,1:T(2,128)(2,1)S(1)}, bf16[1024,1]{0,1:T(2,128)(2,1)}, u32[]{:S(2)}) copy-start(bf16[1024,1]{0,1:T(2,128)(2,1)} %param.40) | copy-start | bytes 6148
  13.6 29.2 %all-to-all-start.1 = ((bf16[32,96,128]{2,1,0:T(8,128)(2,1)}), bf16[32,96,128]{2,1,0:T(8,128)(2,1)S(1)}, u32[]{:S(2)}, u32[]{:S(2)}) async-start(bf16[32,96,128]{2,1,0:T(8,128)(2,1)} %bitcast.21), calls=%async_computation.1 | async-start | bytes 1572864 | tf_op jit(solution)/shard_map/all_to_all | solution.py:260
  42.8 1.1 copy-start
  57.6 9.7 %all-to-all-start.2 = ((f32[32,1,128]{2,1,0:T(1,128)}), f32[32,1,128]{2,1,0:T(1,128)S(1)}, u32[]{:S(2)}, u32[]{:S(2)}) async-start(f32[32,1,128]{2,1,0:T(1,128)} %bitcast.25), calls=%async_computation.2 | async-start | bytes 32768 | tf_op jit(solution)/shard_map/all_to_all | solution.py:275
  67.3 52.6 %all-to-all-start = ((bf16[64,128,128]{2,1,0:T(8,128)(2,1)}), bf16[64,128,128]{2,1,0:T(8,128)(2,1)S(1)}, u32[]{:S(2)}, u32[]{:S(2)}) async-start(bf16[64,128,128]{2,1,0:T(8,128)(2,1)} %place.1), calls=%async_computation | async-start | bytes 4194304 | tf_op jit(solution)/shard_map/all_to_all | solution.py:249

commit v2 on v1

--- a/solution.py
+++ b/solution.py
@@ -7,6 +7,7 @@
 from jax.experimental.pallas import tpu as pltpu
 from jax.sharding import PartitionSpec as P
 
+
 F = 26
 SLAB = 32
 VM = pltpu.VMEM
@@ -25,33 +26,66 @@
     return jnp.dot(a, b, preferred_element_type=F32)
 
 
-def place_kernel(slots, owner_ref, blocks_ref, out_ref, used):
-    chips = out_ref.shape[0] // slots
-    out_ref[...] = jnp.zeros_like(out_ref)
+def place_kernel(me_ref, owner_ref, blocks_ref, *rest):
+    outs, buf, used = rest[:-2], rest[-2], rest[-1]
+    chips, slots = len(outs), outs[0].shape[0]
+    buf[...] = jnp.zeros_like(buf)
     for c in range(chips):
         used[c] = 0
 
     def step(i, carry):
-        c = owner_ref[i]
+        c = lax.rem(owner_ref[i] - me_ref[0] + chips, chips)
         rank = used[c]
         used[c] = rank + 1
-        out_ref[c * slots + rank] = blocks_ref[i]
+        buf[c * slots + rank] = blocks_ref[i]
         return carry
 
     lax.fori_loop(0, blocks_ref.shape[0], step, 0)
-
-
-def place(owners, blocks, chips, slots):
-    shape = (chips * slots,) + blocks.shape[1:]
+    for k, out in enumerate(outs):
+        out[...] = buf[k * slots:(k + 1) * slots]
+
+
+def place(me, owners, blocks, chips, slots):
+    shape = (slots,) + blocks.shape[1:]
+    smem, vmem = pl.BlockSpec(memory_space=pltpu.SMEM), pl.BlockSpec(memory_space=VM)
     return pl.pallas_call(
-        functools.partial(place_kernel, slots),
-        out_shape=jax.ShapeDtypeStruct(shape, blocks.dtype),
-        in_specs=[pl.BlockSpec(memory_space=pltpu.SMEM), pl.BlockSpec(memory_space=VM)],
-        out_specs=pl.BlockSpec(memory_space=VM),
-        scratch_shapes=[pltpu.SMEM((chips,), I32)],
+        place_kernel,
+        out_shape=[jax.ShapeDtypeStruct(shape, blocks.dtype)] * chips,
+        in_specs=[smem, smem, vmem],
+        out_specs=[vmem] * chips,
+        scratch_shapes=[VM((chips * slots,) + blocks.shape[1:], blocks.dtype), pltpu.SMEM((chips,), I32)],
         cost_estimate=cost(1000, 3 * blocks.size * 2),
+        compiler_params=pltpu.CompilerParams(vmem_limit_bytes=12 * 2**20),
         name="place",
-    )(owners, blocks)
+    )(me, owners, blocks)
+
+
+def gather_kernel(me_ref, *rest):
+    ins, out_ref, sems = rest[:-2], rest[-2], rest[-1]
+    chips, slots = len(ins), ins[0].shape[0]
+    copies = []
+    for k, ref in enumerate(ins):
+        holder = lax.rem(me_ref[0] - k + chips, chips)
+        copies.append(pltpu.make_async_copy(ref, out_ref.at[pl.ds(holder * slots, slots)], sems.at[k]))
+    for copy in copies:
+        copy.start()
+    for copy in copies:
+        copy.wait()
+
+
+def gather(me, parts):
+    shape = (len(parts) * parts[0].shape[0],) + parts[0].shape[1:]
+    vmem = pl.BlockSpec(memory_space=VM)
+    return pl.pallas_call(
+        gather_kernel,
+        out_shape=jax.ShapeDtypeStruct(shape, parts[0].dtype),
+        in_specs=[pl.BlockSpec(memory_space=pltpu.SMEM)] + [vmem] * len(parts),
+        out_specs=pl.BlockSpec(memory_space=pl.ANY),
+        scratch_shapes=[pltpu.SemaphoreType.DMA((len(parts),))],
+        cost_estimate=cost(1000, 4 * len(parts) * parts[0].size),
+        compiler_params=pltpu.CompilerParams(vmem_limit_bytes=8 * 2**20),
+        name="gather",
+    )(me, *parts)
 
 
 def pool_kernel(peers, stride, off_ref, samp_ref, home_ref, orph_ref, out_ref, rows_ref):
@@ -93,6 +127,7 @@
         out_specs=pl.BlockSpec(memory_space=VM),
         scratch_shapes=[VM((peers * stride, width), F32)],
         cost_estimate=cost(2 * peers * (home.size + orph.size), 4 * home.size),
+        compiler_params=pltpu.CompilerParams(vmem_limit_bytes=20 * 2**20),
         name="pool",
     )(off, samp, home, orph)
 
@@ -208,6 +243,7 @@
             VM((SLAB * SLAB, wt.shape[1]), BF16),
         ],
         cost_estimate=cost(8_000_000_000, 8_000_000),
+        compiler_params=pltpu.CompilerParams(vmem_limit_bytes=44 * 2**20),
         name="top",
     )(arrived, samp, dense, w1, b1, w2, b2, w3, b3, wt, bh, wl, bl, labels)
 
@@ -240,13 +276,24 @@
     everyone = ("hst", "chip")
     homes, orphs = resident_row_blocks.shape[0], orphan_blocks.shape[0]
     height, width = resident_row_blocks.shape[1:]
-    batch = dense_inputs.shape[0]
     slots = (2 * orphs + chips - 1) // chips
     count = homes + orphs
-    stride = -(-(count + 2) // 16) * 16
-
-    outgoing = place(orphan_owner[:, 0], orphan_blocks, chips, slots)
-    rehomed = lax.all_to_all(outgoing, "chip", split_axis=0, concat_axis=0, tiled=True)
+    stride = -(-(count + 2) // 8) * 8
+
+    me = lax.axis_index("chip")[None].astype(I32)
+    parts = list(place(me, orphan_owner[:, 0], orphan_blocks, chips, slots))
+
+    def send(shifts):
+        for k in shifts:
+            parts[k] = lax.ppermute(parts[k], "chip", [(c, (c + k) % chips) for c in range(chips)])
+
+    order = sorted(range(1, chips), key=lambda k: abs(2 * k - chips))
+    load, early = 0, []
+    while 2.2 * (load + min(order[0], chips - order[0])) <= chips * chips // 4:
+        k = order.pop(0)
+        load += min(k, chips - k)
+        early.append(k)
+    send(early)
 
     offsets = jnp.concatenate([home_offsets, orphan_offsets], axis=0)
     lengths = jnp.concatenate([home_lengths, orphan_lengths], axis=0)
@@ -259,6 +306,12 @@
     packed = packed.reshape(devices, stride, width)
     arrived = lax.all_to_all(packed, everyone, split_axis=0, concat_axis=0, tiled=True)
 
+    held = lax.optimization_barrier((arrived, [parts[k] for k in order]))
+    arrived = held[0]
+    for k, part in zip(order, held[1]):
+        parts[k] = part
+    send(order)
+
     total = devices * count
     depth = -(-total // (F * 128)) * 128
     where = (arrived[:, count, :count].astype(F32) * 256.0
@@ -272,6 +325,7 @@
         bottom_third, bias_third[None], top_hidden, bias_hidden[None],
         top_logit.T.astype(F32), bias_logit, labels[None],
     )
+    rehomed = gather(me, parts)
     losses = lax.all_to_all(loss[:, None, :], everyone, split_axis=0, concat_axis=0, tiled=True)
     return rehomed, logits[0], jnp.sum(losses[:, 0, 0])
 
@@ -279,6 +333,7 @@
 def solution(mesh):
     both = ("hst", "chip")
     three, two = P(both, None, None), P(both, None)
+
     return jax.shard_map(
         per_device,
         mesh=mesh,

time: 122 us -> 96.7 us (0.79)
  waiting for transfers between devices: 72.1 us -> 24.6 us
  blocking collectives: 0 us -> 23.1 us
  starting transfers between devices: 13.4 us -> 18.4 us
  Pallas kernels: 23.1 us -> 19.5 us
  local copies, waits for them, and re-layouts: 7.3 us -> 5.76 us
    all_to_all x2 -> x0, waiting for transfers between devices: 52.3 us -> none  [the longest x1 48.3 us: per_device(): lax.all_to_all(outgoing, 'chip', split_axis=0, concat_axis=0, tiled=True)]
    all_to_all x0 -> x1, blocking collectives: none -> 23.1 us  [per_device(): lax.all_to_all(loss[:, None, :], everyone, split_axis=0, concat_axis=0, t...]
    ppermute x0 -> x7, starting transfers between devices: none -> 11.1 us  [send(): lax.ppermute(parts[k], 'chip', [(c, (c + k) % chips) for c in range(chips)])]
    all_to_all x2 -> x0, starting transfers between devices: 6.11 us -> none  [the longest x1 3.61 us: per_device(): lax.all_to_all(outgoing, 'chip', split_axis=0, concat_axis=0, tiled=True)]
    all_to_all x1, waiting for transfers between devices: 19.8 us -> 24 us  [per_device(): lax.all_to_all(packed, everyone, split_axis=0, concat_axis=0, tiled=True)]
    pallas_call x1, Pallas kernels: 6.19 us -> 3.89 us  [pool(): pl.pallas_call(functools.partial(pool_kernel, peers, stride), out_shape=j...]
    pallas_call x1, Pallas kernels: 13.8 us -> 12 us  [top(): pl.pallas_call(functools.partial(top_kernel, homes, orphs, depth), out_sh...]
    pallas_call x1 -> x2, Pallas kernels: 3.18 us -> 3.53 us  [the longest x1 2.15 us: place(): pl.pallas_call(place_kernel, out_shape=[jax.ShapeDtypeStruct(shape, block...]
  transfers between devices with their start and end apart: 3 -> 8, of which waited for: 3 -> 2; matrix products, arithmetic and copies ran while one was open for 2% -> 1% of each run, Pallas kernels for 3% -> 15%
where the time goes in v2:
time: 96.7 us; the launch traced here: 96.1 us
  waiting for transfers between devices  24.6 us (25%)
  blocking collectives  23.1 us (24%)
  Pallas kernels  19.5 us (20%)
  starting transfers between devices  18.4 us (19%)
  local copies, waits for them, and re-layouts  5.76 us (6%)
  other arithmetic  3.28 us (3%)
  between operations  1.52 us (2%)
    all_to_all x1, waiting for transfers between devices, per_device(): lax.all_to_all(packed, everyone, split_axis=0, concat_axis=0, tiled=True)  24 us
    all_to_all x1, blocking collectives, per_device(): lax.all_to_all(loss[:, None, :], everyone, split_axis=0, concat_axis=0, t...  23.1 us
    pallas_call x1, Pallas kernels, top(): pl.pallas_call(functools.partial(top_kernel, homes, orphs, depth), out_sh...  12 us
    ppermute x7, starting transfers between devices, send(): lax.ppermute(parts[k], 'chip', [(c, (c + k) % chips) for c in range(chips)])  11.1 us
    all_to_all x1, starting transfers between devices, per_device(): lax.all_to_all(packed, everyone, split_axis=0, concat_axis=0, tiled=True)  7.33 us
    unnamed x42, local copies, waits for them, and re-layouts  5.01 us
    pallas_call x1, Pallas kernels, pool(): pl.pallas_call(functools.partial(pool_kernel, peers, stride), out_shape=j...  3.89 us
    pallas_call x1, Pallas kernels, place(): pl.pallas_call(place_kernel, out_shape=[jax.ShapeDtypeStruct(shape, block...  2.15 us
  transfers between devices with their start and end apart: 8, of which 2 were waited for; matrix products, arithmetic and copies ran while one was open for 1% of the time, Pallas kernels for 15%

profile of v2, /device:TPU:0, one launch (start us, length us, event | category | flops | bytes accessed | tf_op | source)
XLA Modules:
  0.0 96.1 jit_solution(1222729149492763695)
XLA Ops:
  0.6 0.9 copy.35
  1.5 0.8 copy.38
  2.3 1.0 %copy.36 = s32[32,32,8]{0,2,1:T(8,128)S(1)} copy(s32[32,32,8]{1,2,0:T(8,128)} %param.26) | data formatting | bytes 65536 | tf_op args[5]
  3.3 0.8 pad_add_fusion
  4.1 1.0 %fusion = s32[8,80,32]{1,0,2:T(8,128)S(1)} fusion(s32[32,32,8]{0,2,1:T(8,128)S(1)} %copy.36, s32[48,32,8]{0,2,1:T(8,128)} %param.23, s32[80,32]{0,1:T(8,128)S(1)} %pad_add_fusion), kind=kLoop, calls=%fused_computation.1 | loop fusion | flops 61440 | bytes 174080 | tf_op jit(solution)/shard_map/transpose | solution.py:302
  5.1 0.2 copy.37
  5.3 0.2 reshape.42.off_ref
  5.5 0.8 add_bitcast_fusion
  6.3 1.4 %copy-done.1 = bf16[48,128,128]{2,1,0:T(8,128)(2,1)S(1)} copy-done((bf16[48,128,128]{2,1,0:T(8,128)(2,1)S(1)}, bf16[48,128,128]{2,1,0:T(8,128)(2,1)}, u32[]{:S(2)}) %copy-start.1) | copy-done | bytes 1572888
  7.7 3.9 %pool.1 = bf16[2816,128]{1,0:T(8,128)(2,1)} custom-call(s32[8,2560]{1,0:T(8,128)S(1)} %reshape.42.off_ref, s32[32,128]{1,0:T(8,128)S(1)} %pad.8.samp_ref, bf16[48,128,128]{2,1,0:T(8,128)(2,1)S(1)} %copy-done.1, bf16[32,128,128]{2,1,0:T(8,128)(2,1)S(1)} %copy-done), custom_call_target="tpu_custom_call" | custom-call | flops 83886080 | bytes 3145728 | tf_op jit(solution)/shard_map/pool/pallas_call | solution.py:123
  11.7 7.3 %all-to-all-start = ((bf16[32,88,128]{2,1,0:T(8,128)(2,1)}), bf16[32,88,128]{2,1,0:T(8,128)(2,1)S(1)}, u32[]{:S(2)}, u32[]{:S(2)}) async-start(bf16[32,88,128]{2,1,0:T(8,128)(2,1)} %bitcast.4), calls=%async_computation | async-start | bytes 1441792 | tf_op jit(solution)/shard_map/all_to_all | solution.py:307
  19.0 2.1 %place.1 = (bf16[8,128,128]{2,1,0:T(8,128)(2,1)S(1)}, bf16[8,128,128]{2,1,0:T(8,128)(2,1)S(1)}, bf16[8,128,128]{2,1,0:T(8,128)(2,1)S(1)}, bf16[8,128,128]{2,1,0:...) custom-call(s32[1]{0:T(128)} %bitcast.me_ref, ...), custom_call_target="tpu_custom_call" | custom-call | flops 1000 | bytes 3145728 | tf_op jit(solution)/shard_map/place/pallas_call | solution.py:51
  21.2 0.7 copy-done.9
  21.9 1.5 %collective-permute-start.2 = (bf16[8,128,128]{2,1,0:T(8,128)(2,1)}, bf16[8,128,128]{2,1,0:T(8,128)(2,1)S(1)}, u32[]{:S(2)}, u32[]{:S(2)}) collective-permute-start(bf16[8,128,128]{2,1,0:T(8,128)(2,1)} %get-tuple-element.27), channel_id=1, source_target_pairs={{0,3},{1,4},{2,5},{3,6},{4,7},{5,0},{6,1},{7,2},{8,11},{9,12},{10,... | collective-permute-start | bytes 786440 | tf_op jit(solution)/shard_map/ppermute | solution.py:288
  23.4 2.4 %collective-permute-start.3 = (bf16[8,128,128]{2,1,0:T(8,128)(2,1)}, bf16[8,128,128]{2,1,0:T(8,128)(2,1)S(1)}, u32[]{:S(2)}, u32[]{:S(2)}) collective-permute-start(bf16[8,128,128]{2,1,0:T(8,128)(2,1)} %get-tuple-element.28), channel_id=1, source_target_pairs={{0,4},{1,5},{2,6},{3,7},{4,0},{5,1},{6,2},{7,3},{8,12},{9,13},{10,... | collective-permute-start | bytes 786440 | tf_op jit(solution)/shard_map/ppermute | solution.py:288
  26.5 0.2 copy.40.dense_ref
  26.7 24.0 %all-to-all-done.arr_ref = bf16[32,88,128]{2,1,0:T(8,128)(2,1)S(1)} async-done(((bf16[32,88,128]{2,1,0:T(8,128)(2,1)}), bf16[32,88,128]{2,1,0:T(8,128)(2,1)S(1)}, u32[]{:S(2)}, u32[]{:S(2)}) %all-to-all-start) | async-done | bytes 720928 | tf_op jit(solution)/shard_map/all_to_all | solution.py:307
  51.3 3.7 %collective-permute-start.4 = (bf16[8,128,128]{2,1,0:T(8,128)(2,1)}, bf16[8,128,128]{2,1,0:T(8,128)(2,1)S(1)}, u32[]{:S(2)}, u32[]{:S(2)}) collective-permute-start(bf16[8,128,128]{2,1,0:T(8,128)(2,1)} %copy-done.7), channel_id=1, source_target_pairs={{0,5},{1,6},{2,7},{3,0},{4,1},{5,2},{6,3},{7,4},{8,13},{9,14},{10,... | collective-permute-start | bytes 786440 | tf_op jit(solution)/shard_map/ppermute | solution.py:288
  55.1 0.6 collective-permute-done.3.rest_4_
  55.7 3.1 %collective-permute-start.6 = (bf16[8,128,128]{2,1,0:T(8,128)(2,1)}, bf16[8,128,128]{2,1,0:T(8,128)(2,1)S(1)}, u32[]{:S(2)}, u32[]{:S(2)}) collective-permute-start(bf16[8,128,128]{2,1,0:T(8,128)(2,1)} %copy-done.5), channel_id=1, source_target_pairs={{0,7},{1,0},{2,1},{3,2},{4,3},{5,4},{6,5},{7,6},{8,15},{9,8},{10,9... | collective-permute-start | bytes 786440 | tf_op jit(solution)/shard_map/ppermute | solution.py:288
  58.9 12.0 %top.1 = (f32[1,512]{1,0:T(1,128)}, f32[32,128]{1,0:T(8,128)S(1)}) custom-call(bf16[32,88,128]{2,1,0:T(8,128)(2,1)S(1)} %all-to-all-done.arr_ref, s32[26,128]{1,0:T(8,128)S(1)} %bitcast.22, bf16[512,13]{1,0:T(8,128)(2,1)S(1)} %copy.40.dense_ref, bf16[13,512]{1,0:T(8,128)(2,1)S(1)} %copy-done.11, f32[1,512]{1,0:T(1,128)S(1)} %bitcast.26, ...), custom_call_target="tpu_custom_call" | custom-call | flops 8000000000 | bytes 8000000 | tf_op jit(solution)/shard_map/top/pallas_call | solution.py:230
  70.9 23.1 %all_to_all.10 = f32[32,1,128]{2,1,0:T(1,128)S(1)} all-to-all(f32[32,1,128]{2,1,0:T(1,128)S(1)} %bitcast.23), channel_id=1, replica_groups=mesh['hst'=4,'chip'=8] {'hst','chip'}, dimensions={0} | all-to-all | bytes 32768 | tf_op jit(solution)/shard_map/all_to_all | solution.py:329
  94.1 0.6 slice_reduce_fusion
  94.8 1.4 %gather.1 = bf16[64,128,128]{2,1,0:T(8,128)(2,1)} custom-call(s32[1]{0:T(128)} %bitcast.me_ref, bf16[8,128,128]{2,1,0:T(8,128)(2,1)S(1)} %get-tuple-element.19.rest_0_, bf16[8,128,128]{2,1,0:T(8,128)(2,1)S(1)} %collective-permute-done.rest_1_, bf16[8,128,128]{2,1,0:T(8,128)(2,1)S(1)} %collective-permute-done.1.rest_2_, ...), custom_call_target="tpu_custom_call" | custom-call | flops 1000 | bytes 4194304 | tf_op jit(solution)/shard_map/gather/pallas_call | solution.py:79
  (55 shorter events, 0.8 us)
Async XLA Ops:
  0.6 5.6 %copy-start = (bf16[32,128,128]{2,1,0:T(8,128)(2,1)S(1)}, bf16[32,128,128]{2,1,0:T(8,128)(2,1)}, u32[]{:S(2)}) copy-start(bf16[32,128,128]{2,1,0:T(8,128)(2,1)} %orph_ref.1) | copy-start | bytes 3145732
  7.7 11.3 %copy-start.2 = (s32[32,1]{0,1:T(1,128)S(1)}, s32[32,1]{0,1:T(1,128)}, u32[]{:S(2)}) copy-start(s32[32,1]{0,1:T(1,128)} %param.29) | copy-start | bytes 388
  11.6 14.9 %copy-start.17 = (bf16[512,13]{0,1:T(8,128)(2,1)S(1)}, bf16[512,13]{0,1:T(8,128)(2,1)}, u32[]{:S(2)}) copy-start(bf16[512,13]{0,1:T(8,128)(2,1)} %param.30) | copy-start | bytes 39940
  11.6 15.1 %copy-start.18 = (bf16[1024,1]{0,1:T(2,128)(2,1)S(1)}, bf16[1024,1]{0,1:T(2,128)(2,1)}, u32[]{:S(2)}) copy-start(bf16[1024,1]{0,1:T(2,128)(2,1)} %param.40) | copy-start | bytes 6148
  11.6 47.3 %copy-start.3 = (bf16[479,1024]{1,0:T(8,128)(2,1)S(1)}, bf16[479,1024]{1,0:T(8,128)(2,1)}, u32[]{:S(2)}) copy-start(bf16[479,1024]{1,0:T(8,128)(2,1)} %wt_ref.1) | copy-start | bytes 2942980
  11.6 47.3 %copy-start.4 = (bf16[512,256]{1,0:T(8,128)(2,1)S(1)}, bf16[512,256]{1,0:T(8,128)(2,1)}, u32[]{:S(2)}) copy-start(bf16[512,256]{1,0:T(8,128)(2,1)} %w2_ref.1) | copy-start | bytes 786436
  11.6 47.3 %copy-start.10 = (bf16[256,128]{1,0:T(8,128)(2,1)S(1)}, bf16[256,128]{1,0:T(8,128)(2,1)}, u32[]{:S(2)}) copy-start(bf16[256,128]{1,0:T(8,128)(2,1)} %w3_ref.1) | copy-start | bytes 196612
  11.6 47.3 %copy-start.11 = (bf16[13,512]{1,0:T(8,128)(2,1)S(1)}, bf16[13,512]{1,0:T(8,128)(2,1)}, u32[]{:S(2)}) copy-start(bf16[13,512]{1,0:T(8,128)(2,1)} %w1_ref.1) | copy-start | bytes 39940
  11.6 47.3 %copy-start.12 = (f32[1024]{0:T(1024)S(1)}, f32[1024]{0:T(1024)}, u32[]{:S(2)}) copy-start(f32[1024]{0:T(1024)} %param.39) | copy-start | bytes 12292
  11.6 47.3 %copy-start.13 = (f32[512]{0:T(512)S(1)}, f32[512]{0:T(512)}, u32[]{:S(2)}) copy-start(f32[512]{0:T(512)} %param.33) | copy-start | bytes 6148
  11.6 47.2 %copy-start.14 = (s32[512]{0:T(512)S(1)}, s32[512]{0:T(512)}, u32[]{:S(2)}) copy-start(s32[512]{0:T(512)} %param.31) | copy-start | bytes 6148
  11.6 47.2 %copy-start.15 = (f32[256]{0:T(256)S(1)}, f32[256]{0:T(256)}, u32[]{:S(2)}) copy-start(f32[256]{0:T(256)} %param.35) | copy-start | bytes 3076
  11.7 47.2 %copy-start.16 = (f32[128]{0:T(128)S(1)}, f32[128]{0:T(128)}, u32[]{:S(2)}) copy-start(f32[128]{0:T(128)} %param.37) | copy-start | bytes 1540
  11.7 39.0 %all-to-all-start = ((bf16[32,88,128]{2,1,0:T(8,128)(2,1)}), bf16[32,88,128]{2,1,0:T(8,128)(2,1)S(1)}, u32[]{:S(2)}, u32[]{:S(2)}) async-start(bf16[32,88,128]{2,1,0:T(8,128)(2,1)} %bitcast.4), calls=%async_computation | async-start | bytes 1441792 | tf_op jit(solution)/shard_map/all_to_all | solution.py:307
  21.9 4.0 %copy-start.6 = (bf16[8,128,128]{2,1,0:T(8,128)(2,1)}, bf16[8,128,128]{2,1,0:T(8,128)(2,1)S(1)}, u32[]{:S(2)}) copy-start(bf16[8,128,128]{2,1,0:T(8,128)(2,1)S(1)} %get-tuple-element.30) | copy-start | bytes 786436
  21.9 4.0 %copy-start.7 = (bf16[8,128,128]{2,1,0:T(8,128)(2,1)}, bf16[8,128,128]{2,1,0:T(8,128)(2,1)S(1)}, u32[]{:S(2)}) copy-start(bf16[8,128,128]{2,1,0:T(8,128)(2,1)S(1)} %get-tuple-element.29) | copy-start | bytes 786436
  21.9 4.0 %copy-start.8 = (bf16[8,128,128]{2,1,0:T(8,128)(2,1)}, bf16[8,128,128]{2,1,0:T(8,128)(2,1)S(1)}, u32[]{:S(2)}) copy-start(bf16[8,128,128]{2,1,0:T(8,128)(2,1)S(1)} %get-tuple-element.26) | copy-start | bytes 786436
  21.9 33.2 %collective-permute-start.2 = (bf16[8,128,128]{2,1,0:T(8,128)(2,1)}, bf16[8,128,128]{2,1,0:T(8,128)(2,1)S(1)}, u32[]{:S(2)}, u32[]{:S(2)}) collective-permute-start(bf16[8,128,128]{2,1,0:T(8,128)(2,1)} %get-tuple-element.27), channel_id=1, source_target_pairs={{0,3},{1,4},{2,5},{3,6},{4,7},{5,0},{6,1},{7,2},{8,11},{9,12},{10,... | collective-permute-start | bytes 786440 | tf_op jit(solution)/shard_map/ppermute | solution.py:288
  23.4 32.3 %collective-permute-start.3 = (bf16[8,128,128]{2,1,0:T(8,128)(2,1)}, bf16[8,128,128]{2,1,0:T(8,128)(2,1)S(1)}, u32[]{:S(2)}, u32[]{:S(2)}) collective-permute-start(bf16[8,128,128]{2,1,0:T(8,128)(2,1)} %get-tuple-element.28), channel_id=1, source_target_pairs={{0,4},{1,5},{2,6},{3,7},{4,0},{5,1},{6,2},{7,3},{8,12},{9,13},{10,... | collective-permute-start | bytes 786440 | tf_op jit(solution)/shard_map/ppermute | solution.py:288
  51.2 43.6 %collective-permute-start = (bf16[8,128,128]{2,1,0:T(8,128)(2,1)}, bf16[8,128,128]{2,1,0:T(8,128)(2,1)S(1)}, u32[]{:S(2)}, u32[]{:S(2)}) collective-permute-start(bf16[8,128,128]{2,1,0:T(8,128)(2,1)} %copy-done.9), channel_id=1, source_target_pairs={{0,1},{1,2},{2,3},{3,4},{4,5},{5,6},{6,7},{7,0},{8,9},{9,10},{10,1... | collective-permute-start | bytes 786440 | tf_op jit(solution)/shard_map/ppermute | solution.py:288
  51.3 43.4 %collective-permute-start.1 = (bf16[8,128,128]{2,1,0:T(8,128)(2,1)}, bf16[8,128,128]{2,1,0:T(8,128)(2,1)S(1)}, u32[]{:S(2)}, u32[]{:S(2)}) collective-permute-start(bf16[8,128,128]{2,1,0:T(8,128)(2,1)} %copy-done.8), channel_id=1, source_target_pairs={{0,2},{1,3},{2,4},{3,5},{4,6},{5,7},{6,0},{7,1},{8,10},{9,11},{10,... | collective-permute-start | bytes 786440 | tf_op jit(solution)/shard_map/ppermute | solution.py:288
  51.3 43.4 %collective-permute-start.4 = (bf16[8,128,128]{2,1,0:T(8,128)(2,1)}, bf16[8,128,128]{2,1,0:T(8,128)(2,1)S(1)}, u32[]{:S(2)}, u32[]{:S(2)}) collective-permute-start(bf16[8,128,128]{2,1,0:T(8,128)(2,1)} %copy-done.7), channel_id=1, source_target_pairs={{0,5},{1,6},{2,7},{3,0},{4,1},{5,2},{6,3},{7,4},{8,13},{9,14},{10,... | collective-permute-start | bytes 786440 | tf_op jit(solution)/shard_map/ppermute | solution.py:288
  55.0 39.7 %collective-permute-start.5 = (bf16[8,128,128]{2,1,0:T(8,128)(2,1)}, bf16[8,128,128]{2,1,0:T(8,128)(2,1)S(1)}, u32[]{:S(2)}, u32[]{:S(2)}) collective-permute-start(bf16[8,128,128]{2,1,0:T(8,128)(2,1)} %copy-done.6), channel_id=1, source_target_pairs={{0,6},{1,7},{2,0},{3,1},{4,2},{5,3},{6,4},{7,5},{8,14},{9,15},{10,... | collective-permute-start | bytes 786440 | tf_op jit(solution)/shard_map/ppermute | solution.py:288
  55.7 39.0 %collective-permute-start.6 = (bf16[8,128,128]{2,1,0:T(8,128)(2,1)}, bf16[8,128,128]{2,1,0:T(8,128)(2,1)S(1)}, u32[]{:S(2)}, u32[]{:S(2)}) collective-permute-start(bf16[8,128,128]{2,1,0:T(8,128)(2,1)} %copy-done.5), channel_id=1, source_target_pairs={{0,7},{1,0},{2,1},{3,2},{4,3},{5,4},{6,5},{7,6},{8,15},{9,8},{10,9... | collective-permute-start | bytes 786440 | tf_op jit(solution)/shard_map/ppermute | solution.py:288
  (3 other events, 6.1 us)
